TPU v7x, 32 devices: a whole 2x2x4 slice. The times are simulated.
32 devices in a mesh: grp: 8 (over z, x), vocab: 4 (over y, core).
Axes of the slice: x: 2, y: 2, z: 4, core: 2. Of those that a mesh axis runs over, the one named last changes fastest.
Arguments:
- teacher_rows: bfloat16 [64, 8, 4096], P('grp', None, 'vocab'), may hold values from -160 to 160
- student_rows: bfloat16 [8, 32, 5120], P('grp', None, 'vocab'), may hold values from -160 to 160
- teacher_head: bfloat16 [4096, 8192], P(None, ('grp', 'vocab')), may hold values from -0.25 to 0.25
- student_head: bfloat16 [5120, 8192], P(None, ('grp', 'vocab')), may hold values from -0.25 to 0.25
- lengths: int32 [64], replicated, may hold values from 1 to 8, as said below
- owner: int32 [64], replicated, may hold values from 0 to 7, as said below
Outputs:
- divergence: float32 [8, 32], P('grp')
- grad_student: bfloat16 [8, 32, 5120], P('grp', None, 'vocab')
Inputs may be any that keep to these rules, and one draw needn't show every extreme that they name: All 8 sequences of one teacher group share one owner, and each student group owns the sequences of exactly one teacher group. The lengths of the 8 sequences of one teacher group sum to at most 32, and to exactly 32 for some group.
All inputs are finite; a program needn't handle non-finite values.
Results may differ from a plain program's by a relative error of at most 0.018.
Values may be sent and summed in bfloat16 or wider, within the bound.
A program may use at most 64 MiB of HBM per device.

v0:
```python
import jax
import jax.numpy as jnp
from jax import lax
from jax.sharding import PartitionSpec as P


def routing_tables(lengths, owner, groups, seq_count, positions, pad_rows):
    slot_count = seq_count * positions
    group_ids = jnp.arange(groups, dtype=jnp.int32)
    length_table = lengths.reshape(groups, seq_count)
    owner_table = owner.reshape(groups, seq_count)[:, 0]
    teacher_of = jnp.sum(
        (owner_table[None, :] == group_ids[:, None]).astype(jnp.int32) * group_ids[None, :], axis=1
    )
    position_ids = jnp.arange(positions, dtype=jnp.int32)
    live_slots = (position_ids[None, None, :] < length_table[:, :, None]).reshape(
        groups, slot_count
    )
    ranked = jnp.cumsum(live_slots.astype(jnp.int32), axis=1) - 1
    target = jnp.where(live_slots, ranked, pad_rows)
    matches = target[:, None, :] == jnp.arange(pad_rows, dtype=jnp.int32)[None, :, None]
    source = jnp.sum(
        matches.astype(jnp.int32) * jnp.arange(slot_count, dtype=jnp.int32)[None, None, :], axis=2
    )
    totals = jnp.sum(length_table, axis=1)
    owned_total = jnp.take(totals, teacher_of, axis=0)
    student_live = jnp.arange(pad_rows, dtype=jnp.int32)[None, :] < owned_total[:, None]
    return (teacher_of, source, student_live)


def per_device(teacher_rows, student_rows, teacher_head, student_head, lengths, owner):
    groups = lax.axis_size("grp")
    seq_count = teacher_rows.shape[0]
    positions = teacher_rows.shape[1]
    slot_count = seq_count * positions
    pad_rows = student_rows.shape[1]
    own_group = lax.axis_index("grp")
    teacher_of, source, student_live = routing_tables(
        lengths, owner, groups, seq_count, positions, pad_rows
    )
    local_teacher = teacher_rows.reshape(slot_count, teacher_rows.shape[2])
    local_student = student_rows.reshape(pad_rows, student_rows.shape[2])
    own_source = lax.dynamic_index_in_dim(source, own_group, 0, keepdims=False)
    sent_teacher = jnp.take(local_teacher, own_source, axis=0)
    row_position = teacher_of[:, None] * pad_rows + jnp.arange(pad_rows, dtype=jnp.int32)[None, :]
    teacher_full, student_full = (
        lax.all_gather(sent_teacher, "vocab", axis=1, tiled=True),
        lax.all_gather(local_student, "vocab", axis=1, tiled=True),
    )
    raw_teacher = jnp.dot(
        lax.all_gather(teacher_full, "grp", axis=0, tiled=True),
        teacher_head,
        preferred_element_type=jnp.float32,
    )
    student_logits = jnp.dot(
        lax.all_gather(student_full, "grp", axis=0, tiled=True),
        student_head,
        preferred_element_type=jnp.float32,
    )
    teacher_logits = jnp.take(raw_teacher, row_position.reshape(-1), axis=0)
    weight = student_live.reshape(-1).astype(jnp.float32)
    teacher_top, student_top = lax.pmax(
        (jnp.max(teacher_logits, axis=1), jnp.max(student_logits, axis=1)), ("grp", "vocab")
    )
    teacher_total, student_total = lax.psum(
        (
            jnp.sum(jnp.exp(teacher_logits - teacher_top[:, None]), axis=1),
            jnp.sum(jnp.exp(student_logits - student_top[:, None]), axis=1),
        ),
        ("grp", "vocab"),
    )
    teacher_lse = teacher_top + jnp.log(teacher_total)
    student_lse = student_top + jnp.log(student_total)
    log_q = student_logits - student_lse[:, None]
    log_p = teacher_logits - teacher_lse[:, None]
    student_prob = jnp.exp(log_q)
    log_ratio = log_q - log_p
    kl_rows = lax.psum(jnp.sum(student_prob * log_ratio, axis=1), ("grp", "vocab"))
    kl_rows = kl_rows * weight
    grad_logits = (weight[:, None] * student_prob * (log_ratio - kl_rows[:, None])).astype(
        jnp.bfloat16
    )
    partial_value = jnp.einsum(
        "rv,dv->rd", grad_logits, student_head, preferred_element_type=jnp.float32
    )
    feature_totals_acc = lax.psum_scatter(
        partial_value.astype(jnp.bfloat16), "vocab", scatter_dimension=1, tiled=True
    )
    grad_rows = lax.psum_scatter(feature_totals_acc, "grp", scatter_dimension=0, tiled=True)
    divergence = lax.dynamic_slice_in_dim(kl_rows, own_group * pad_rows, pad_rows, 0)
    return (divergence.reshape(1, pad_rows), grad_rows.reshape(1, pad_rows, grad_rows.shape[1]))


def solution(mesh):
    placed = (
        P("grp", None, "vocab"),
        P("grp", None, "vocab"),
        P(None, ("grp", "vocab")),
        P(None, ("grp", "vocab")),
        P(),
        P(),
    )
    return jax.shard_map(
        per_device,
        mesh=mesh,
        in_specs=placed,
        out_specs=(P("grp", None), P("grp", None, "vocab")),
        check_vma=False,
    )
```

profile of v0, /device:TPU:0, one launch (start us, length us, event | category | flops | bytes accessed | tf_op | source)
XLA Modules:
  0.0 356.8 jit_solution(3793422730505756832)
XLA Ops:
  7.2 0.0 copy-start
  7.2 0.0 all-gather.5.cloned.1.call-start
  7.2 0.9 reshape.194
  8.1 0.1 lt.122
  8.2 0.1 lt.124
  8.3 0.1 lt.125
  8.4 0.2 reduce_window_sum.11
  8.6 0.2 select_reduce_fusion.1
  8.9 1.6 gather_fusion.1
  10.5 0.1 broadcast_select_fusion
  10.5 7.7 %all_gather.14 = bf16[32,4096]{1,0:T(8,128)(2,1)} all-gather(bf16[32,1024]{1,0:T(8,128)(2,1)S(1)} %broadcast_select_fusion), channel_id=1, replica_groups=mesh['grp'=8,'vocab'=4] {'vocab'}, dimensions={1}, use_global_device_ids=true | all-gather | bytes 327680 | tf_op jit(solution)/shard_map/all_gather | solution.py:47
  18.2 0.0 all-gather.5.cloned.1.call-update
  18.3 0.0 all-gather.7.cloned.1.call-start
  18.3 8.2 %all-gather = bf16[1,32,5120]{2,1,0:T(8,128)(2,1)} all-gather(bf16[1,32,1280]{2,1,0:T(8,128)(2,1)} %param.7), channel_id=2, replica_groups=mesh['grp'=8,'vocab'=4] {'vocab'}, dimensions={2}, use_global_device_ids=true | all-gather | bytes 409600 | tf_op jit(solution)/shard_map/all_gather | solution.py:48
  26.5 0.0 all-gather.7.cloned.1.call-update
  26.5 0.0 reduce-scatter.3.cloned.1.call-start
  26.6 0.1 reduce_sum.57
  26.7 0.7 reshape.193
  27.4 0.1 slice_reduce_fusion
  27.5 0.1 select_reduce_fusion.2
  27.7 0.6 gather_fusion
  28.3 0.1 iota_add_fusion
  28.4 0.1 add.134
  28.5 0.1 add.126
  28.6 0.1 iota_compare_fusion.2
  28.6 0.1 lt.118
  28.8 40.1 %all-gather.5.cloned.1.call-done = bf16[256,4096]{1,0:T(8,128)(2,1)} async-done(((bf16[32,4096]{1,0:T(8,128)(2,1)}), bf16[256,4096]{1,0:T(8,128)(2,1)}) %all-gather.5.cloned.1.call-update) | async-done | bytes 2097168 | tf_op jit(solution)/shard_map/all_gather | solution.py:51
  68.9 2.9 fusion.13
  71.8 1.0 gather_fusion.2
  72.8 0.1 copy.10
  72.9 0.1 select_reduce_fusion
  73.0 51.0 %all-gather.7.cloned.1.call-done = bf16[1,256,5120]{2,1,0:T(8,128)(2,1)} async-done(((bf16[1,32,5120]{2,1,0:T(8,128)(2,1)}), bf16[1,256,5120]{2,1,0:T(8,128)(2,1)}) %all-gather.7.cloned.1.call-update) | async-done | bytes 2621456 | tf_op jit(solution)/shard_map/all_gather | solution.py:56
  124.0 0.0 copy-done
  124.0 2.9 fusion.12
  126.9 39.3 %all-reduce.1 = (f32[256]{0:T(256)S(1)}, f32[256]{0:T(256)S(1)}) all-reduce(f32[256]{0:T(256)S(1)} %select_reduce_fusion, f32[256]{0:T(256)S(1)} %get-tuple-element.10), channel_id=1, replica_groups=mesh['grp'=8,'vocab'=4] {'grp','vocab'}, use_global_device_ids=true, to_apply=%region_9.10 | all-reduce | flops 512 | bytes 4096 | tf_op jit(solution)/shard_map/pmax | solution.py:62
  166.2 0.1 exponential_reduce_fusion
  166.3 39.9 %all-reduce = (f32[256]{0:T(256)S(1)}, f32[256]{0:T(256)S(1)}) all-reduce(f32[256]{0:T(256)S(1)} %get-tuple-element.12, f32[256]{0:T(256)S(1)} %get-tuple-element.13), channel_id=1, replica_groups=mesh['grp'=8,'vocab'=4] {'grp','vocab'}, use_global_device_ids=true, to_apply=%region_11.12 | all-reduce | flops 512 | bytes 4096 | tf_op jit(solution)/shard_map/psum | solution.py:65
  206.2 0.1 multiply_reduce_fusion
  206.3 40.1 %psum.23 = f32[256]{0:T(256)S(1)} all-reduce(f32[256]{0:T(256)S(1)} %multiply_reduce_fusion), channel_id=1, replica_groups=mesh['grp'=8,'vocab'=4] {'grp','vocab'}, use_global_device_ids=true, to_apply=%region_13.14 | all-reduce | flops 256 | bytes 2048 | tf_op jit(solution)/shard_map/psum | solution.py:78
  246.4 2.4 convolution_convert_fusion
  248.8 0.0 reduce-scatter.3.cloned.1.call-update
  248.9 0.0 reduce-scatter.5.cloned.1.call-start
  248.9 34.8 %reduce-scatter.3.cloned.1.call-done = bf16[256,1280]{1,0:T(8,128)(2,1)} async-done(((bf16[256,5120]{1,0:T(8,128)(2,1)}), bf16[256,1280]{1,0:T(8,128)(2,1)}) %reduce-scatter.3.cloned.1.call-update) | async-done | bytes 655376 | tf_op jit(solution)/shard_map/reduce_scatter | solution.py:86
  283.7 0.0 reduce-scatter.5.cloned.1.call-update
  283.7 0.6 dynamic-slice_bitcast_fusion
  284.3 65.9 %reduce-scatter.5.cloned.1.call-done = bf16[32,1280]{1,0:T(8,128)(2,1)} async-done(((bf16[256,1280]{1,0:T(8,128)(2,1)}), bf16[32,1280]{1,0:T(8,128)(2,1)}) %reduce-scatter.5.cloned.1.call-update) | async-done | bytes 81936 | tf_op jit(solution)/shard_map/reduce_scatter | solution.py:89
  (16 shorter events, 0.1 us)
Async XLA Ops:
  7.2 116.9 %copy-start = (bf16[5120,256]{1,0:T(8,128)(2,1)S(1)}, bf16[5120,256]{1,0:T(8,128)(2,1)}, u32[]{:S(2)}) copy-start(bf16[5120,256]{1,0:T(8,128)(2,1)} %param.9) | copy-start | bytes 7864324
  7.2 61.7 %all-gather.5.cloned.1.call-start = ((), (), s32[]{:S(2)}) async-start(), calls=%async_computation.2 | async-start | bytes 2359296 | tf_op jit(solution)/shard_map/all_gather | solution.py:51
  18.3 105.8 %all-gather.7.cloned.1.call-start = ((), (), s32[]{:S(2)}) async-start(), calls=%async_computation.5 | async-start | bytes 2949120 | tf_op jit(solution)/shard_map/all_gather | solution.py:56
  26.5 257.2 %reduce-scatter.3.cloned.1.call-start = ((), (), s32[]{:S(2)}) async-start(), calls=%async_computation.3 | async-start | bytes 3276800 | tf_op jit(solution)/shard_map/reduce_scatter | solution.py:86
  248.9 101.4 %reduce-scatter.5.cloned.1.call-start = ((), (), s32[]{:S(2)}) async-start(), calls=%async_computation.4 | async-start | bytes 737280 | tf_op jit(solution)/shard_map/reduce_scatter | solution.py:89
Sparse Core Ops, SparseCore 0:
  18.4 50.4 all-gather.4
  71.0 52.9 all-gather.6
  249.0 34.6 reduce-scatter.2
  287.4 62.7 reduce-scatter.4
where the time goes:
time: 357 us
  waiting for transfers between devices  192 us (54%)
  blocking collectives  135 us (38%)
  between operations  13.9 us (4%)
  matrix products  8.25 us (2%)
  local copies, waits for them, and re-layouts  6.15 us (2%)
    reduce_scatter x1, waiting for transfers between devices, per_device(): lax.psum_scatter(feature_totals_acc, 'grp', scatter_dimension=0, tiled=True)  65.9 us
    all_gather x1, waiting for transfers between devices, per_device(): lax.all_gather(student_full, 'grp', axis=0, tiled=True)  51 us
    psum x1, blocking collectives, per_device(): lax.psum(jnp.sum(student_prob * log_ratio, axis=1), ('grp', 'vocab'))  40.1 us
    all_gather x1, waiting for transfers between devices, per_device(): lax.all_gather(teacher_full, 'grp', axis=0, tiled=True)  40.1 us
    psum x1, blocking collectives, per_device(): lax.psum((jnp.sum(jnp.exp(teacher_logits - teacher_top[:, None]), axis=1)...  39.9 us
    pmax x1, blocking collectives, per_device(): lax.pmax((jnp.max(teacher_logits, axis=1), jnp.max(student_logits, axis=1...  39.3 us
    reduce_scatter x1, waiting for transfers between devices, per_device(): lax.psum_scatter(partial_value.astype(jnp.bfloat16), 'vocab', scatter_dim...  34.8 us
    all_gather x1, blocking collectives, per_device(): lax.all_gather(local_student, 'vocab', axis=1, tiled=True)  8.2 us
  transfers between devices with their start and end apart: 4, of which 4 were waited for; matrix products, arithmetic and copies ran while one was open for 2% of the time, Pallas kernels for 0%

commit v1 on v0

v1 whole, which is shorter than its diff:
```python
import functools

import jax
import jax.numpy as jnp
from jax import lax
from jax.experimental import pallas as pl
from jax.experimental.pallas import tpu as pltpu
from jax.sharding import PartitionSpec as P

MESH = pl.DeviceIdType.MESH
PIECES = 8
f32 = jnp.float32


def place():
    g, v = lax.axis_index("grp"), lax.axis_index("vocab")
    return g, v, v // 2, lax.rem(v, 2)


def enter(g, v, peers):
    barrier = pltpu.get_barrier_semaphore()
    for peer in peers:
        pl.semaphore_signal(barrier, inc=1, device_id=peer, device_id_type=MESH)
    pl.semaphore_wait(barrier, len(peers))


def tree_peers(g, v, y, c, groups, lines):
    peers = [(g, v + 1 - 2 * c)]
    peers += [(g, lax.rem(y + j, lines) * 2 + c) for j in range(1, lines)]
    peers += [(lax.rem(g + k, groups), v) for k in range(1, groups)]
    return peers


def send(src, dst, send_sem, recv_sem, device):
    return pltpu.make_async_remote_copy(
        src_ref=src, dst_ref=dst, send_sem=send_sem, recv_sem=recv_sem,
        device_id=device, device_id_type=MESH,
    )


def gather_kernel(groups, lines, pieces, t_in, s_in, t_out, s_out, gs, gr, ys, yr, cs, cr):
    g, v, y, c = place()
    per = groups // pieces
    pairs = ((t_in, t_out), (s_in, s_out))
    for src, out in pairs:
        out[v, g] = src[...]
    enter(g, v, tree_peers(g, v, y, c, groups, lines))
    first = g // per
    across = (g, v + 1 - 2 * c)
    waits = []

    def grp_copy(a, k):
        src, out = pairs[a]
        return send(src, out.at[v, g], gs.at[a, k], gr.at[a, k], (lax.rem(g + k, groups), v))

    def line_copy(a, j, kp):
        out = pairs[a][1]
        piece = out.at[v, pl.ds(lax.rem(first - kp + pieces, pieces) * per, per)]
        return send(piece, piece, ys.at[a, j, kp], yr.at[a, j, kp],
                    (g, lax.rem(y + j, lines) * 2 + c))

    def core_copy(a, j):
        out = pairs[a][1]
        slot = out.at[lax.rem(y - j + lines, lines) * 2 + c]
        return send(slot, slot, cs.at[a, j], cr.at[a, j], across)

    for k in range(1, groups):
        for a in range(2):
            copy = grp_copy(a, k)
            copy.start()
            waits.append(copy)
    for kp in range(pieces):
        for a in range(2):
            for i in range(per):
                block = lax.rem(first - kp + pieces, pieces) * per + i
                k = lax.rem(g - block + groups, groups)

                if per == 1:
                    if kp > 0:
                        grp_copy(a, kp).wait_recv()
                else:
                    @pl.when(k > 0)
                    def _():
                        send(pairs[a][0], pairs[a][1].at[v, g], gs.at[a, k], gr.at[a, k],
                             across).wait_recv()
            for j in range(1, lines):
                copy = line_copy(a, j, kp)
                copy.start()
                waits.append(copy)
    for a in range(2):
        copy = core_copy(a, 0)
        copy.start()
        waits.append(copy)
    for j in range(1, lines):
        for a in range(2):
            for kp in range(pieces):
                line_copy(a, j, kp).wait_recv()
            copy = core_copy(a, j)
            copy.start()
            waits.append(copy)
    for j in range(lines):
        for a in range(2):
            core_copy(a, j).wait_recv()
    for copy in waits:
        copy.wait_send()


def stats_kernel(groups, width, mine, out, gs, gr, vs, vr):
    g, v, _, _ = place()
    out[v, g] = mine[...]
    peers = [(g, lax.rem(v + j, width)) for j in range(1, width)]
    peers += [(lax.rem(g + k, groups), v) for k in range(1, groups)]
    enter(g, v, peers)
    near = [
        send(mine, out.at[v, g], gs.at[k], gr.at[k], (lax.rem(g + k, groups), v))
        for k in range(1, groups)
    ]
    for copy in near:
        copy.start()
    for copy in near:
        copy.wait_recv()
    wide = [
        send(out.at[v], out.at[v], vs.at[j], vr.at[j], (g, lax.rem(v + j, width)))
        for j in range(1, width)
    ]
    for copy in wide:
        copy.start()
    for copy in wide:
        copy.wait_recv()
    for copy in near + wide:
        copy.wait_send()


def scatter_kernel(groups, lines, pieces, part, out, cbuf, ysum, ybuf, gsum, gbuf, acc,
                   cs, cr, ys, yr, gs, gr):
    g, v, y, c = place()
    per = groups // pieces
    first = g // per
    enter(g, v, tree_peers(g, v, y, c, groups, lines))
    other = 1 - c

    def line_of(j):
        return lax.rem(y + j, lines)

    core = [
        send(part.at[line_of(j) * 2 + other], cbuf.at[j], cs.at[j], cr.at[j], (g, v + 1 - 2 * c))
        for j in range(lines)
    ]
    for j in list(range(1, lines)) + [0]:
        core[j].start()
    waits = list(core)
    order = list(range(1, pieces)) + [0]
    line = {}
    for j in range(1, lines):
        core[j].wait_recv()
        for kp in order:
            low = lax.rem(first + kp, pieces) * per
            span = pl.ds(low, per)
            ysum[j, span] = (
                part[line_of(j) * 2 + c, span].astype(f32) + cbuf[j, span].astype(f32)
            ).astype(jnp.bfloat16)
            copy = send(ysum.at[j, span], ybuf.at[j, span], ys.at[j, kp], yr.at[j, kp],
                        (g, line_of(j) * 2 + c))
            copy.start()
            line[j, kp] = copy
            waits.append(copy)
    core[0].wait_recv()

    def total(block):
        value = part[v, block].astype(f32) + cbuf[0, block].astype(f32)
        for j in range(1, lines):
            value = value + ybuf[j, block].astype(f32)
        return value

    def far(k, device):
        return send(gsum.at[k], gbuf.at[k], gs.at[k], gr.at[k], device)

    for kp in order:
        for j in range(1, lines):
            line[j, kp].wait_recv()
        for i in range(per):
            block = lax.rem(first + kp, pieces) * per + i
            k = lax.rem(block - g + groups, groups)
            if per == 1:
                if kp == 0:
                    acc[...] = total(g)
                else:
                    gsum[kp] = total(block).astype(jnp.bfloat16)
                    far(kp, (block, v)).start()
            else:
                @pl.when(k == 0)
                def _():
                    acc[...] = total(block)

                @pl.when(k > 0)
                def _():
                    gsum[k] = total(block).astype(jnp.bfloat16)
                    far(k, (block, v)).start()
    value = acc[...]
    for k in range(1, groups):
        far(k, (lax.rem(g + k, groups), v)).wait_recv()
        value = value + gbuf[k].astype(f32)
    out[...] = value.astype(jnp.bfloat16)
    for copy in waits:
        copy.wait_send()
    for k in range(1, groups):
        far(k, (lax.rem(g + k, groups), v)).wait_send()


VM = pl.BlockSpec(memory_space=pltpu.VMEM)
DMA = pltpu.SemaphoreType.DMA


def params(number):
    return pltpu.CompilerParams(
        collective_id=number, has_side_effects=True, vmem_limit_bytes=48 * 1024 * 1024
    )


def per_device(teacher_rows, student_rows, teacher_head, student_head, lengths, owner):
    groups, width = lax.axis_size("grp"), lax.axis_size("vocab")
    lines = width // 2
    pieces = PIECES if groups % PIECES == 0 else groups
    seqs, positions, dt = teacher_rows.shape
    _, pad, ds = student_rows.shape
    slots, rows, vocab = seqs * positions, groups * pad, teacher_head.shape[1]
    own = lax.axis_index("grp")
    ids = jnp.arange(groups, dtype=jnp.int32)
    table = lengths.reshape(groups, seqs)
    owned = owner.reshape(groups, seqs)[:, 0][None, :] == ids[:, None]
    totals = jnp.sum(table, axis=1)
    live = jnp.arange(pad, dtype=jnp.int32)[None, :] < jnp.sum(
        jnp.where(owned, totals[None, :], 0), axis=1
    )[:, None]
    mine = lax.dynamic_index_in_dim(table, own, 0, keepdims=False)
    seq_ids = jnp.arange(seqs, dtype=jnp.int32)
    starts = jnp.sum(jnp.where(seq_ids[None, :] < seq_ids[:, None], mine[None, :], 0), axis=1)
    pos = jnp.arange(positions, dtype=jnp.int32)
    target = jnp.where(pos[None, :] < mine[:, None], starts[:, None] + pos[None, :], -1)
    target = target.reshape(slots)
    k_ids = jnp.arange(pad, dtype=jnp.int32)
    pick = (target[None, :] == k_ids[:, None]) | (
        (k_ids[:, None] >= jnp.sum(mine)) & (jnp.arange(slots)[None, :] == 0)
    )
    sent = jnp.dot(
        pick.astype(jnp.bfloat16), teacher_rows.reshape(slots, dt), preferred_element_type=f32
    ).astype(jnp.bfloat16)

    t_all, s_all = pl.pallas_call(
        functools.partial(gather_kernel, groups, lines, pieces),
        out_shape=(
            jax.ShapeDtypeStruct((width, groups, pad, dt), jnp.bfloat16),
            jax.ShapeDtypeStruct((width, groups, pad, ds), jnp.bfloat16),
        ),
        in_specs=[VM, VM],
        out_specs=(VM, VM),
        scratch_shapes=[
            DMA((2, groups)), DMA((2, groups)),
            DMA((2, lines, pieces)), DMA((2, lines, pieces)),
            DMA((2, lines)), DMA((2, lines)),
        ],
        compiler_params=params(0),
    )(sent, student_rows.reshape(pad, ds))

    raw = jnp.einsum(
        "vrd,vdn->rn", t_all.reshape(width, rows, dt), teacher_head.reshape(width, dt, vocab),
        preferred_element_type=f32,
    ).reshape(groups, pad, vocab)
    head = student_head.reshape(width, ds, vocab)
    s = jnp.einsum("vrd,vdn->rn", s_all.reshape(width, rows, ds), head, preferred_element_type=f32)
    t = jnp.sum(jnp.where(owned[:, :, None, None], raw[None], 0.0), axis=1).reshape(rows, vocab)

    t_top, s_top = jnp.max(t, axis=1), jnp.max(s, axis=1)
    s_exp = jnp.exp(s - s_top[:, None])
    zero = jnp.zeros((rows,), f32)
    stats = jnp.stack([
        t_top, jnp.sum(jnp.exp(t - t_top[:, None]), axis=1),
        s_top, jnp.sum(s_exp, axis=1), jnp.sum(s_exp * (s - t), axis=1), zero, zero, zero,
    ])
    every = pl.pallas_call(
        functools.partial(stats_kernel, groups, width),
        out_shape=jax.ShapeDtypeStruct((width, groups, 8, rows), f32),
        in_specs=[VM],
        out_specs=VM,
        scratch_shapes=[DMA((groups,)), DMA((groups,)), DMA((width,)), DMA((width,))],
        compiler_params=params(1),
    )(stats).reshape(width * groups, 8, rows)
    t_max, s_max = jnp.max(every[:, 0], axis=0), jnp.max(every[:, 2], axis=0)
    s_scale = jnp.exp(every[:, 2] - s_max)
    t_lse = t_max + jnp.log(jnp.sum(every[:, 1] * jnp.exp(every[:, 0] - t_max), axis=0))
    s_total = jnp.sum(every[:, 3] * s_scale, axis=0)
    s_lse = s_max + jnp.log(s_total)
    cross = jnp.sum(every[:, 4] * s_scale, axis=0) / s_total
    weight = live.reshape(-1).astype(f32)
    kl = (cross - (s_lse - t_lse)) * weight
    log_q = s - s_lse[:, None]
    log_p = t - t_lse[:, None]
    grad = (weight[:, None] * jnp.exp(log_q) * (log_q - log_p - kl[:, None])).astype(jnp.bfloat16)
    part = jnp.einsum("rn,vdn->vrd", grad, head, preferred_element_type=f32).astype(jnp.bfloat16)
    block = (groups, pad, ds)
    out = pl.pallas_call(
        functools.partial(scatter_kernel, groups, lines, pieces),
        out_shape=jax.ShapeDtypeStruct((pad, ds), jnp.bfloat16),
        in_specs=[VM],
        out_specs=VM,
        scratch_shapes=[
            pltpu.VMEM((lines,) + block, jnp.bfloat16),
            pltpu.VMEM((lines,) + block, jnp.bfloat16),
            pltpu.VMEM((lines,) + block, jnp.bfloat16),
            pltpu.VMEM(block, jnp.bfloat16),
            pltpu.VMEM(block, jnp.bfloat16),
            pltpu.VMEM((pad, ds), f32),
            DMA((lines,)), DMA((lines,)),
            DMA((lines, pieces)), DMA((lines, pieces)),
            DMA((groups,)), DMA((groups,)),
        ],
        compiler_params=params(2),
    )(part.reshape((width,) + block))
    divergence = lax.dynamic_slice_in_dim(kl, own * pad, pad, 0)
    return divergence.reshape(1, pad), out.reshape(1, pad, ds)


def solution(mesh):
    placed = (
        P("grp", None, "vocab"),
        P("grp", None, "vocab"),
        P(None, ("grp", "vocab")),
        P(None, ("grp", "vocab")),
        P(),
        P(),
    )
    return jax.shard_map(
        per_device,
        mesh=mesh,
        in_specs=placed,
        out_specs=(P("grp", None), P("grp", None, "vocab")),
        check_vma=False,
    )
```

time: 357 us -> 100 us (0.28)
  waiting for transfers between devices: 192 us -> 0 us
  blocking collectives: 135 us -> 0 us
  Pallas kernels: 0 us -> 83.3 us
  between operations: 13.9 us -> 0.79 us
    reduce_scatter x2 -> x0, waiting for transfers between devices: 101 us -> none  [the longest x1 65.9 us: per_device(): lax.psum_scatter(feature_totals_acc, 'grp', scatter_dimension=0, tiled=True)]
    all_gather x2 -> x0, waiting for transfers between devices: 91.1 us -> none  [the longest x1 51 us: per_device(): lax.all_gather(student_full, 'grp', axis=0, tiled=True)]
    pallas_call x0 -> x3, Pallas kernels: none -> 83.3 us  [the longest x1 42.4 us: per_device(): pl.pallas_call(functools.partial(gather_kernel, groups, lines, pieces), o...]
    psum x2 -> x0, blocking collectives: 80 us -> none  [the longest x1 40.1 us: per_device(): lax.psum(jnp.sum(student_prob * log_ratio, axis=1), ('grp', 'vocab'))]
    pmax x1 -> x0, blocking collectives: 39.3 us -> none  [per_device(): lax.pmax((jnp.max(teacher_logits, axis=1), jnp.max(student_logits, axis=1...]
    all_gather x2 -> x0, blocking collectives: 15.9 us -> none  [the longest x1 8.2 us: per_device(): lax.all_gather(local_student, 'vocab', axis=1, tiled=True)]
    dot_general x3 -> x4, matrix products: 8.25 us -> 7.2 us  [the longest x1 2.88 us: per_device(): jnp.einsum('vrd,vdn->rn', s_all.reshape(width, rows, ds), head, preferred...]
  transfers between devices with their start and end apart: 4 -> 0, of which waited for: 4 -> 0; matrix products, arithmetic and copies ran while one was open for 2% -> 0% of each run, Pallas kernels for 0% -> 0%
where the time goes in v1:
time: 100 us; the launch traced here: 99.7 us
  Pallas kernels  83.3 us (83%)
  matrix products  7.2 us (7%)
  local copies, waits for them, and re-layouts  5.84 us (6%)
  other arithmetic  2.64 us (3%)
    pallas_call x1, Pallas kernels, per_device(): pl.pallas_call(functools.partial(gather_kernel, groups, lines, pieces), o...  42.4 us
    pallas_call x1, Pallas kernels, per_device(): pl.pallas_call(functools.partial(scatter_kernel, groups, lines, pieces),...  25.7 us
    pallas_call x1, Pallas kernels, per_device(): pl.pallas_call(functools.partial(stats_kernel, groups, width), out_shape=...  15.1 us
    unnamed x7, local copies, waits for them, and re-layouts  3.03 us
    dot_general x1, matrix products, per_device(): jnp.einsum('vrd,vdn->rn', s_all.reshape(width, rows, ds), head, preferred...  2.88 us
    dot_general x1, matrix products, per_device(): jnp.einsum('vrd,vdn->rn', t_all.reshape(width, rows, dt), teacher_head.re...  2.29 us

profile of v1, /device:TPU:0, one launch (start us, length us, event | category | flops | bytes accessed | tf_op | source)
XLA Modules:
  0.0 99.7 jit_solution(7678891062438747467)
XLA Ops:
  0.6 0.0 copy-start
  0.6 0.9 reshape.177
  1.5 0.1 reduce_sum.99
  1.6 0.7 reshape.176
  2.4 0.1 slice_reduce_fusion
  2.5 0.1 select_reduce_fusion.2
  2.6 0.1 iota_compare_fusion.4
  2.7 0.1 lt.67
  2.8 0.6 fusion.28
  3.4 0.1 select_reduce_fusion.1
  3.5 0.1 add_select_fusion
  3.6 0.1 select_n.33
  3.7 0.7 iota_compare_fusion.6
  4.4 1.1 %convolution_convert_fusion.1.t_in = bf16[32,1024]{1,0:T(8,128)(2,1)S(1)} fusion(bf16[8,8,1024]{2,1,0:T(8,128)(2,1)} %param.6, s32[64]{0:T(128)S(1)} %select_n.33, pred[64]{0:T(512)(128)(4,1)S(1)} %iota_compare_fusion.5, pred[32]{0:T(512)(128)(4,1)S(1)} %iota_compare_fusion.6), kind=kOutput, calls=%fused_computation.6 | convolution fusion | flops 4233216 | bytes 196960 | tf_op jit(solution)/shard_map/dot_general | solution.py:245
  5.5 0.0 copy-start.2
  5.5 0.9 copy-done.2
  6.4 42.4 %shard_map.77 = (bf16[4,8,32,1024]{3,2,1,0:T(8,128)(2,1)S(1)}, bf16[4,8,32,1280]{3,2,1,0:T(8,128)(2,1)S(1)}) custom-call(bf16[32,1024]{1,0:T(8,128)(2,1)S(1)} %convolution_convert_fusion.1.t_in, bf16[32,1280]{1,0:T(8,128)(2,1)S(1)} %bitcast.82), custom_call_target="tpu_custom_call" | custom-call | tf_op jit(solution)/shard_map/pallas_call | solution.py:249
  48.8 0.0 copy-start.1
  48.8 1.5 %copy-done.1 = bf16[4,8,32,1280]{3,2,1,0:T(8,128)(2,1)} copy-done((bf16[4,8,32,1280]{3,2,1,0:T(8,128)(2,1)}, bf16[4,8,32,1280]{3,2,1,0:T(8,128)(2,1)S(1)}, u32[]{:S(2)}) %copy-start.1) | copy-done | bytes 2621464
  50.3 2.3 %fusion.2 = f32[8,32,256]{2,1,0:T(8,128)S(1)} fusion(bf16[4,1024,256,1]{2,1,3,0:T(8,128)(2,1)} %bitcast.84, bf16[4,8,32,1024]{3,2,1,0:T(8,128)(2,1)S(1)} %get-tuple-element.4), kind=kOutput, calls=%fused_computation.5 | convolution fusion | flops 536870912 | bytes 4456448 | tf_op jit(solution)/shard_map/vrd,vdn->rn/dot_general | solution.py:265
  52.6 0.2 select_reduce_fusion
  52.9 0.1 reduce_max.36
  53.0 0.1 stack.21
  53.1 0.2 exponential_reduce_fusion
  53.3 0.1 stack.22
  53.4 0.0 copy-done
  53.4 2.9 %fusion.30 = (f32[256]{0:T(256)S(1)}, f32[256,256]{0,1:T(8,128)S(1)}) fusion(bf16[4,256,1280]{2,1,0:T(8,128)(2,1)} %bitcast.79, bf16[4,1280,256]{2,1,0:T(8,128)(2,1)S(1)} %bitcast.76), kind=kOutput, calls=%fused_computation.56 | convolution fusion | flops 671153920 | bytes 5506048 | tf_op jit(solution)/shard_map/vrd,vdn->rn/dot_general | solution.py:270
  56.2 0.1 copy.22
  56.4 0.1 multiply_reduce_fusion
  56.5 15.1 %shard_map.78 = f32[4,8,8,256]{3,2,1,0:T(8,128)S(1)} custom-call(f32[8,256]{1,0:T(8,128)S(1)} %stack.27.mine), custom_call_target="tpu_custom_call" | custom-call | tf_op jit(solution)/shard_map/pallas_call | solution.py:280
  71.6 0.1 slice_reduce_fusion.1
  71.8 0.6 dynamic-slice_bitcast_fusion
  72.4 0.9 convolution_convert_fusion
  73.3 25.7 %shard_map.79 = bf16[32,1280]{1,0:T(8,128)(2,1)S(1)} custom-call(bf16[4,8,32,1280]{3,2,1,0:T(8,128)(2,1)S(1)} %bitcast.78), custom_call_target="tpu_custom_call" | custom-call | tf_op jit(solution)/shard_map/pallas_call | solution.py:301
  99.1 0.6 copy.65
  (8 shorter events, 0.1 us)
Async XLA Ops:
  0.6 52.7 %copy-start = (bf16[5120,256]{1,0:T(8,128)(2,1)S(1)}, bf16[5120,256]{1,0:T(8,128)(2,1)}, u32[]{:S(2)}) copy-start(bf16[5120,256]{1,0:T(8,128)(2,1)} %param.9) | copy-start | bytes 7864324
  5.5 0.9 copy-start.2
  48.8 1.5 %copy-start.1 = (bf16[4,8,32,1280]{3,2,1,0:T(8,128)(2,1)}, bf16[4,8,32,1280]{3,2,1,0:T(8,128)(2,1)S(1)}, u32[]{:S(2)}) copy-start(bf16[4,8,32,1280]{3,2,1,0:T(8,128)(2,1)S(1)} %get-tuple-element.5) | copy-start | bytes 7864324

commit v2 on v1

--- a/solution.py
+++ b/solution.py
@@ -59,10 +59,11 @@
         return send(piece, piece, ys.at[a, j, kp], yr.at[a, j, kp],
                     (g, lax.rem(y + j, lines) * 2 + c))
 
-    def core_copy(a, j):
+    def core_copy(a, j, kp):
         out = pairs[a][1]
-        slot = out.at[lax.rem(y - j + lines, lines) * 2 + c]
-        return send(slot, slot, cs.at[a, j], cr.at[a, j], across)
+        slot = out.at[lax.rem(y - j + lines, lines) * 2 + c,
+                      pl.ds(lax.rem(first - kp + pieces, pieces) * per, per)]
+        return send(slot, slot, cs.at[a, j, kp], cr.at[a, j, kp], across)
 
     for k in range(1, groups):
         for a in range(2):
@@ -87,20 +88,20 @@
                 copy = line_copy(a, j, kp)
                 copy.start()
                 waits.append(copy)
-    for a in range(2):
-        copy = core_copy(a, 0)
-        copy.start()
-        waits.append(copy)
-    for j in range(1, lines):
-        for a in range(2):
-            for kp in range(pieces):
-                line_copy(a, j, kp).wait_recv()
-            copy = core_copy(a, j)
+            copy = core_copy(a, 0, kp)
             copy.start()
             waits.append(copy)
+    for j in range(1, lines):
+        for kp in range(pieces):
+            for a in range(2):
+                line_copy(a, j, kp).wait_recv()
+                copy = core_copy(a, j, kp)
+                copy.start()
+                waits.append(copy)
     for j in range(lines):
-        for a in range(2):
-            core_copy(a, j).wait_recv()
+        for kp in range(pieces):
+            for a in range(2):
+                core_copy(a, j, kp).wait_recv()
     for copy in waits:
         copy.wait_send()
 
@@ -257,7 +258,7 @@
         scratch_shapes=[
             DMA((2, groups)), DMA((2, groups)),
             DMA((2, lines, pieces)), DMA((2, lines, pieces)),
-            DMA((2, lines)), DMA((2, lines)),
+            DMA((2, lines, pieces)), DMA((2, lines, pieces)),
         ],
         compiler_params=params(0),
     )(sent, student_rows.reshape(pad, ds))

time: 100 us -> 99.7 us (level)
  no operation moved by 1% of the time
where the time goes in v2:
time: 99.7 us; the launch traced here: 99.5 us
  Pallas kernels  83 us (83%)
  matrix products  7.2 us (7%)
  local copies, waits for them, and re-layouts  5.84 us (6%)
  other arithmetic  2.64 us (3%)
    pallas_call x1, Pallas kernels, per_device(): pl.pallas_call(functools.partial(gather_kernel, groups, lines, pieces), o...  42.1 us
    pallas_call x1, Pallas kernels, per_device(): pl.pallas_call(functools.partial(scatter_kernel, groups, lines, pieces),...  25.8 us
    pallas_call x1, Pallas kernels, per_device(): pl.pallas_call(functools.partial(stats_kernel, groups, width), out_shape=...  15.1 us
    unnamed x7, local copies, waits for them, and re-layouts  3.03 us
    dot_general x1, matrix products, per_device(): jnp.einsum('vrd,vdn->rn', s_all.reshape(width, rows, ds), head, preferred...  2.88 us
    dot_general x1, matrix products, per_device(): jnp.einsum('vrd,vdn->rn', t_all.reshape(width, rows, dt), teacher_head.re...  2.29 us

profile of v2, /device:TPU:0, one launch (start us, length us, event | category | flops | bytes accessed | tf_op | source)
XLA Modules:
  0.0 99.5 jit_solution(7026895161015109004)
XLA Ops:
  0.6 0.0 copy-start
  0.6 0.9 reshape.177
  1.5 0.1 reduce_sum.99
  1.6 0.7 reshape.176
  2.4 0.1 slice_reduce_fusion
  2.5 0.1 select_reduce_fusion.2
  2.6 0.1 iota_compare_fusion.4
  2.7 0.1 lt.67
  2.8 0.6 fusion.28
  3.4 0.1 select_reduce_fusion.1
  3.5 0.1 add_select_fusion
  3.6 0.1 select_n.33
  3.7 0.7 iota_compare_fusion.6
  4.4 1.1 %convolution_convert_fusion.1.t_in = bf16[32,1024]{1,0:T(8,128)(2,1)S(1)} fusion(bf16[8,8,1024]{2,1,0:T(8,128)(2,1)} %param.6, s32[64]{0:T(128)S(1)} %select_n.33, pred[64]{0:T(512)(128)(4,1)S(1)} %iota_compare_fusion.5, pred[32]{0:T(512)(128)(4,1)S(1)} %iota_compare_fusion.6), kind=kOutput, calls=%fused_computation.6 | convolution fusion | flops 4233216 | bytes 196960 | tf_op jit(solution)/shard_map/dot_general | solution.py:246
  5.5 0.0 copy-start.2
  5.5 0.9 copy-done.2
  6.4 42.1 %shard_map.77 = (bf16[4,8,32,1024]{3,2,1,0:T(8,128)(2,1)S(1)}, bf16[4,8,32,1280]{3,2,1,0:T(8,128)(2,1)S(1)}) custom-call(bf16[32,1024]{1,0:T(8,128)(2,1)S(1)} %convolution_convert_fusion.1.t_in, bf16[32,1280]{1,0:T(8,128)(2,1)S(1)} %bitcast.82), custom_call_target="tpu_custom_call" | custom-call | tf_op jit(solution)/shard_map/pallas_call | solution.py:250
  48.5 0.0 copy-start.1
  48.5 1.5 %copy-done.1 = bf16[4,8,32,1280]{3,2,1,0:T(8,128)(2,1)} copy-done((bf16[4,8,32,1280]{3,2,1,0:T(8,128)(2,1)}, bf16[4,8,32,1280]{3,2,1,0:T(8,128)(2,1)S(1)}, u32[]{:S(2)}) %copy-start.1) | copy-done | bytes 2621464
  50.0 2.3 %fusion.2 = f32[8,32,256]{2,1,0:T(8,128)S(1)} fusion(bf16[4,1024,256,1]{2,1,3,0:T(8,128)(2,1)} %bitcast.84, bf16[4,8,32,1024]{3,2,1,0:T(8,128)(2,1)S(1)} %get-tuple-element.4), kind=kOutput, calls=%fused_computation.5 | convolution fusion | flops 536870912 | bytes 4456448 | tf_op jit(solution)/shard_map/vrd,vdn->rn/dot_general | solution.py:266
  52.3 0.2 select_reduce_fusion
  52.6 0.1 reduce_max.36
  52.7 0.1 stack.21
  52.8 0.2 exponential_reduce_fusion
  53.0 0.1 stack.22
  53.1 0.0 copy-done
  53.1 2.9 %fusion.30 = (f32[256]{0:T(256)S(1)}, f32[256,256]{0,1:T(8,128)S(1)}) fusion(bf16[4,256,1280]{2,1,0:T(8,128)(2,1)} %bitcast.79, bf16[4,1280,256]{2,1,0:T(8,128)(2,1)S(1)} %bitcast.76), kind=kOutput, calls=%fused_computation.56 | convolution fusion | flops 671153920 | bytes 5506048 | tf_op jit(solution)/shard_map/vrd,vdn->rn/dot_general | solution.py:271
  55.9 0.1 copy.22
  56.1 0.1 multiply_reduce_fusion
  56.2 15.1 %shard_map.78 = f32[4,8,8,256]{3,2,1,0:T(8,128)S(1)} custom-call(f32[8,256]{1,0:T(8,128)S(1)} %stack.27.mine), custom_call_target="tpu_custom_call" | custom-call | tf_op jit(solution)/shard_map/pallas_call | solution.py:281
  71.3 0.1 slice_reduce_fusion.1
  71.6 0.6 dynamic-slice_bitcast_fusion
  72.2 0.9 convolution_convert_fusion
  73.1 25.8 %shard_map.79 = bf16[32,1280]{1,0:T(8,128)(2,1)S(1)} custom-call(bf16[4,8,32,1280]{3,2,1,0:T(8,128)(2,1)S(1)} %bitcast.78), custom_call_target="tpu_custom_call" | custom-call | tf_op jit(solution)/shard_map/pallas_call | solution.py:302
  98.8 0.6 copy.65
  (8 shorter events, 0.1 us)
Async XLA Ops:
  0.6 52.4 %copy-start = (bf16[5120,256]{1,0:T(8,128)(2,1)S(1)}, bf16[5120,256]{1,0:T(8,128)(2,1)}, u32[]{:S(2)}) copy-start(bf16[5120,256]{1,0:T(8,128)(2,1)} %param.9) | copy-start | bytes 7864324
  5.5 0.9 copy-start.2
  48.5 1.5 %copy-start.1 = (bf16[4,8,32,1280]{3,2,1,0:T(8,128)(2,1)}, bf16[4,8,32,1280]{3,2,1,0:T(8,128)(2,1)S(1)}, u32[]{:S(2)}) copy-start(bf16[4,8,32,1280]{3,2,1,0:T(8,128)(2,1)S(1)} %get-tuple-element.5) | copy-start | bytes 7864324
